TPU v7x, 32 devices: a whole 2x2x4 slice. The times are simulated.
32 devices in a mesh: section: 2 (over core), vocab: 16 (over z, y, x).
Axes of the slice: x: 2, y: 2, z: 4, core: 2. Of those that a mesh axis runs over, the one named last changes fastest.
Arguments:
- hidden_in: bfloat16 [2, 256, 7168], P(None, ('section', 'vocab')), may hold values from -6 to 6
- gain_ffn: float32 [7168], replicated, may hold values from 0.4 to 1.6
- w_gate: bfloat16 [7168, 18432], P(None, ('section', 'vocab')), may hold values from -0.0625 to 0.0625
- w_up: bfloat16 [7168, 18432], P(None, ('section', 'vocab')), may hold values from -0.0625 to 0.0625
- w_down: bfloat16 [18432, 7168], P(('section', 'vocab')), may hold values from -0.046875 to 0.046875
- gain_final: float32 [7168], replicated, may hold values from 0.4 to 1.6
- head_weight: bfloat16 [7168, 129280], P(None, ('section', 'vocab')), may hold values from -4.5 to 4.5
- sampled_ids: int32 [2, 256], replicated, may hold values from 0 to 129279
- seq_ids: int32 [2, 256], P(None, ('section', 'vocab')), may hold values from 0 to 7, never falling along the last dimension, each value on 1 to 128 neighbouring positions
Outputs:
- token_logprob: float32 [2, 256], P(None, ('section', 'vocab'))
- log_norm: float32 [2, 256], P(None, ('section', 'vocab'))
- top_mass: float32 [2, 256], P(None, ('section', 'vocab'))
- seq_logprob: float32 [2, 8], replicated
All inputs are finite; a program needn't handle non-finite values.
Results may differ from a plain program's by a relative error of at most 0.006.
Values may be sent and summed in bfloat16 or wider, within the bound.
No kernel may reach another device: no remote copies, remote signals or barrier semaphores. Data moves between devices by JAX's collectives and lax.ppermute only.
A program may use at most 192 MiB of HBM per device.

v0:
```python
import jax
import jax.numpy as jnp
from jax import lax
from jax.sharding import PartitionSpec as P

SEQS = 8
TOPK = 20
epsilon = 1e-06


def rms_norm(values, scale_gain):
    wide = values.astype(jnp.float32)
    square_mean = jnp.mean(wide * wide, axis=-1, keepdims=True)
    return (wide * lax.rsqrt(square_mean + epsilon) * scale_gain).astype(jnp.bfloat16)


def largest(values):
    return lax.sort(values, dimension=values.ndim - 1)[..., -TOPK:]


def finish(peak_value, sum_total, sampled_logit, leaders_all):
    log_norm = peak_value + jnp.log(sum_total)
    top_mass = jnp.sum(jnp.exp(leaders_all - log_norm[:, None]), axis=1)
    return (sampled_logit - log_norm, log_norm, top_mass)


def combine_sources(pieces):
    maxima, exp_sums, sampled_parts, top_values = pieces
    peak_value = jnp.max(maxima, axis=0)
    sum_total = jnp.sum(exp_sums * jnp.exp(maxima - peak_value[None, :]), axis=0)
    sampled_logit = jnp.sum(sampled_parts, axis=0)
    item_count = top_values.shape[1]
    pooled = jnp.transpose(top_values, (1, 0, 2)).reshape(item_count, -1)
    leaders_all = largest(pooled)
    return finish(peak_value, sum_total, sampled_logit, leaders_all)


def body(hidden_in, gain_ffn, w_gate, w_up, w_down, gain_final, head_weight, sampled_ids, seq_ids):
    row_count = hidden_in.shape[1]
    shard_width = head_weight.shape[1]
    position = lax.axis_index(("section", "vocab"))
    group_count = lax.axis_size(("section", "vocab"))
    columns = lax.broadcasted_iota(jnp.int32, (1, shard_width), 1) + position * shard_width
    logprob_list = []
    norm_list = []
    mass_list = []
    partials = []
    for microbatch in range(hidden_in.shape[0]):
        own_rows = hidden_in[microbatch]
        gathered = lax.all_gather(own_rows, ("section", "vocab"), axis=0, tiled=True)
        normed = rms_norm(gathered, gain_ffn)
        gate_proj = jnp.dot(normed, w_gate, preferred_element_type=jnp.float32)
        up_proj = jnp.dot(normed, w_up, preferred_element_type=jnp.float32)
        hidden_act = (jax.nn.silu(gate_proj) * up_proj).astype(jnp.bfloat16)
        branch = lax.psum(
            jnp.dot(hidden_act, w_down, preferred_element_type=jnp.float32), ("section", "vocab")
        )
        residual = (gathered.astype(jnp.float32) + branch).astype(jnp.bfloat16)
        scaled = rms_norm(residual, gain_final)
        logits = jnp.dot(scaled, head_weight, preferred_element_type=jnp.float32)
        token_ids = sampled_ids[microbatch]
        matches = columns == token_ids[:, None]
        sampled_part = jnp.sum(jnp.where(matches, logits, 0.0), axis=1)
        leaders = largest(logits)
        local_peak = jnp.max(logits, axis=1).reshape(group_count, row_count)
        local_total = jnp.sum(jnp.exp(logits - jnp.max(logits, axis=1)[:, None]), axis=1).reshape(
            group_count, row_count
        )
        sampled_block = sampled_part.reshape(group_count, row_count)
        leader_block = leaders.reshape(group_count, row_count, TOPK)
        token_logprob, log_norm, top_mass = combine_sources(
            (
                lax.all_to_all(
                    local_peak, ("section", "vocab"), split_axis=0, concat_axis=0, tiled=True
                ),
                lax.all_to_all(
                    local_total, ("section", "vocab"), split_axis=0, concat_axis=0, tiled=True
                ),
                lax.all_to_all(
                    sampled_block, ("section", "vocab"), split_axis=0, concat_axis=0, tiled=True
                ),
                lax.all_to_all(
                    leader_block, ("section", "vocab"), split_axis=0, concat_axis=0, tiled=True
                ),
            )
        )
        onehot = (
            seq_ids[microbatch][:, None] == jnp.arange(SEQS, dtype=jnp.int32)[None, :]
        ).astype(jnp.float32)
        partials.append(jnp.sum(token_logprob[:, None] * onehot, axis=0))
        logprob_list.append(token_logprob)
        norm_list.append(log_norm)
        mass_list.append(top_mass)
    seq_logprob = lax.psum(jnp.stack(partials), ("section", "vocab"))
    return (jnp.stack(logprob_list), jnp.stack(norm_list), jnp.stack(mass_list), seq_logprob)


def solution(mesh):
    in_specs = (
        P(None, ("section", "vocab"), None),
        P(),
        P(None, ("section", "vocab")),
        P(None, ("section", "vocab")),
        P(("section", "vocab"), None),
        P(),
        P(None, ("section", "vocab")),
        P(),
        P(None, ("section", "vocab")),
    )
    out_specs = (
        P(None, ("section", "vocab")),
        P(None, ("section", "vocab")),
        P(None, ("section", "vocab")),
        P(),
    )
    return jax.shard_map(body, mesh=mesh, in_specs=in_specs, out_specs=out_specs, check_vma=False)
```

profile of v0, /device:TPU:0, one launch (start us, length us, event | category | flops | bytes accessed | tf_op | source)
XLA Modules:
  0.0 1247.0 jit_solution(10427038897527076204)
XLA Ops:
  7.2 1.6 fusion.44
  8.9 0.7 all-gather.7.cloned.1.call-update
  9.7 64.3 %all-gather.5.cloned.1.call-done = bf16[1,256,7168]{2,1,0:T(8,128)(2,1)} async-done(((bf16[1,8,7168]{2,1,0:T(8,128)(2,1)}), bf16[1,256,7168]{2,1,0:T(8,128)(2,1)}) %all-gather.5.cloned.1.call-update) | async-done | bytes 3670032 | tf_op jit(solution)/shard_map/all_gather | solution.py:50
  74.0 2.8 fusion.6
  76.9 59.1 %all-gather.7.cloned.1.call-done = bf16[1,256,7168]{2,1,0:T(8,128)(2,1)} async-done(((bf16[1,8,7168]{2,1,0:T(8,128)(2,1)}), bf16[1,256,7168]{2,1,0:T(8,128)(2,1)}) %all-gather.7.cloned.1.call-update) | async-done | bytes 3670032 | tf_op jit(solution)/shard_map/all_gather | solution.py:50
  135.9 3.0 fusion.10
  139.0 7.0 fusion.28
  146.0 2.4 fusion.25
  148.5 19.7 %fusion.34 = f32[256,7168]{1,0:T(8,128)} fusion(bf16[576,7168]{1,0:T(8,128)(2,1)} %param.13, bf16[7168,576]{0,1:T(8,128)(2,1)} %param.12, bf16[1,256,7168]{2,1,0:T(8,128)(2,1)} %all-gather.5.cloned.1.call-done, f32[7168]{0:T(1024)S(1)} %copy-done.3, f32[256]{0:T(256)S(1)} %add_rsqrt_fusion.3, f32[256,576]{0,1:T(8,128)S(1)} %fusion.28), kind=kOutput, calls=%fused_computation.41 | convolution fusion | flops 4236083200 | bytes 28144640 | tf_op jit(solution)/shard_map/dot_general | solution.py:56
  168.2 19.3 %fusion.31 = f32[256,7168]{1,0:T(8,128)} fusion(bf16[576,7168]{1,0:T(8,128)(2,1)} %param.13, bf16[7168,576]{0,1:T(8,128)(2,1)} %param.12, bf16[1,256,7168]{2,1,0:T(8,128)(2,1)} %all-gather.7.cloned.1.call-done, f32[256]{0:T(256)S(1)} %add_rsqrt_fusion.1, f32[7168]{0:T(1024)S(1)} %copy-done.3, f32[256,576]{0,1:T(8,128)S(1)} %fusion.25), kind=kOutput, calls=%fused_computation.40 | convolution fusion | flops 4236083200 | bytes 28144640 | tf_op jit(solution)/shard_map/dot_general | solution.py:56
  188.2 251.1 %all-reduce.3.cloned.1.call-done = (f32[256,7168]{1,0:T(8,128)}, f32[256,7168]{1,0:T(8,128)}) async-done(((f32[256,7168]{1,0:T(8,128)}, f32[256,7168]{1,0:T(8,128)}), (f32[256,7168]{1,0:T(8,128)}, f32[256,7168]{1,0:T(8,128)})) %all-reduce.3.cloned.1.call-update) | async-done | bytes 14680080 | tf_op jit(solution)/shard_map/psum | solution.py:55
  439.3 8.4 fusion
  447.7 28.2 %fusion.46 = (f32[256]{0:T(256)S(1)}, f32[256,4040]{0,1:T(8,128)}) fusion(bf16[7168,4040]{0,1:T(8,128)(2,1)} %param.15, f32[7168]{0:T(1024)S(1)} %copy-done.4, f32[256]{0:T(256)S(1)} %add_rsqrt_fusion.2, f32[256,7168]{1,0:T(8,128)} %get-tuple-element.25, bf16[1,256,7168]{2,1,0:T(8,128)(2,1)} %all-gather.5.cloned.1.call-done), kind=kOutput, calls=%fused_computation.75 | convolution fusion | flops 14840743936 | bytes 73095168 | tf_op jit(solution)/shard_map/dot_general | solution.py:60
  475.9 0.7 all_to_all.52
  476.6 4.8 all-to-all-start.1
  481.3 2.3 iota.24.clone
  483.6 296.8 %sort.56 = (f32[256,4040]{0,1:T(8,128)}, s32[256,4040]{0,1:T(8,128)}) sort(f32[256,4040]{0,1:T(8,128)} %get-tuple-element.39, s32[256,4040]{0,1:T(8,128)} %iota.24.clone), dimensions={1}, to_apply=%region_18.19 | sort | flops 20684800 | bytes 16547840 | tf_op jit(solution)/shard_map/sort | solution.py:18
  780.4 5.6 copy.39
  786.0 28.4 %fusion.47 = (f32[256]{0:T(256)S(1)}, f32[256,4040]{0,1:T(8,128)}) fusion(bf16[7168,4040]{0,1:T(8,128)(2,1)} %param.15, f32[256]{0:T(256)S(1)} %add_rsqrt_fusion, f32[7168]{0:T(1024)S(1)} %copy-done.4, f32[256,7168]{1,0:T(8,128)} %get-tuple-element.24, bf16[1,256,7168]{2,1,0:T(8,128)(2,1)} %all-gather.7.cloned.1.call-done), kind=kOutput, calls=%fused_computation.76 | convolution fusion | flops 14840743936 | bytes 73095168 | tf_op jit(solution)/shard_map/dot_general | solution.py:60
  814.3 5.1 exponential_reduce_fusion.1
  819.4 1.0 slice_bitcast_fusion.1
  820.4 296.9 %sort.58 = (f32[256,4040]{0,1:T(8,128)}, s32[256,4040]{0,1:T(8,128)}) sort(f32[256,4040]{0,1:T(8,128)} %get-tuple-element.41, s32[256,4040]{0,1:T(8,128)} %iota.24.clone), dimensions={1}, to_apply=%region_21.22 | sort | flops 20684800 | bytes 16547840 | tf_op jit(solution)/shard_map/sort | solution.py:18
  1117.3 0.7 all_to_all.54
  1117.9 5.5 copy.43
  1123.5 5.9 all-to-all-start.2
  1129.4 1.0 slice_bitcast_fusion
  1130.4 0.7 all_to_all.60
  1131.1 0.7 all_to_all.50
  1131.8 0.8 reshape.189
  1132.6 0.7 all_to_all.62
  1133.3 0.7 all_to_all.58
  1134.0 0.7 reshape.187
  1134.7 1.8 all-to-all-done.2
  1136.6 4.0 all-to-all-start
  1140.6 7.1 all-to-all-done
  1147.8 2.5 all-to-all-start.4
  1150.3 7.1 all-to-all-done.4
  1157.4 2.5 all-to-all-start.5
  1160.0 7.1 all-to-all-done.5
  1167.1 2.5 all-to-all-start.3
  1169.6 7.1 all-to-all-done.3
  1176.7 2.5 all-to-all-start.6
  1180.6 40.4 %psum.23 = f32[2,8]{1,0:T(2,128)} all-reduce(f32[2,8]{1,0:T(2,128)S(1)} %pad_maximum_fusion.3), channel_id=1, replica_groups=mesh['section'=2,'vocab'=16] {'section','vocab'}, use_global_device_ids=true, to_apply=%region_26.27 | all-reduce | flops 16 | bytes 128 | tf_op jit(solution)/shard_map/psum | solution.py:94
  1221.0 5.0 all-to-all-start.7
  1226.6 0.7 reduce.5
  1227.6 4.9 sort.57
  1233.3 0.7 reduce.4
  1234.3 4.9 sort.59
  (57 shorter events, 5.0 us)
Async XLA Ops:
  7.2 131.8 %copy-start.3 = (f32[7168]{0:T(1024)S(1)}, f32[7168]{0:T(1024)}, u32[]{:S(2)}) copy-start(f32[7168]{0:T(1024)} %param.10) | copy-start | bytes 86020
  7.2 66.8 %all-gather.5.cloned.1.call-start = ((), (), s32[]{:S(2)}) async-start(), calls=%async_computation.8 | async-start | bytes 3784704 | tf_op jit(solution)/shard_map/all_gather | solution.py:50
  8.9 127.0 %all-gather.7.cloned.1.call-start = ((), (), s32[]{:S(2)}) async-start(), calls=%async_computation.9 | async-start | bytes 3784704 | tf_op jit(solution)/shard_map/all_gather | solution.py:50
  9.6 429.6 %all-reduce.3.cloned.1.call-start = ((), (), s32[]{:S(2)}) async-start(), calls=%async_computation.10 | async-start | bytes 29360128 | tf_op jit(solution)/shard_map/psum | solution.py:55
  135.9 10.1 slice-start
  138.9 7.1 copy-start
  139.0 7.1 slice-start.1
  187.5 0.7 copy-start.2
  187.5 0.7 copy-start.1
  439.3 8.4 copy-start.4
  476.6 646.9 %all-to-all-start.1 = ((f32[32,1,8]{2,1,0:T(1,128)}), f32[32,1,8]{2,1,0:T(1,128)S(1)}, u32[]{:S(2)}, u32[]{:S(2)}) async-start(f32[32,1,8]{2,1,0:T(1,128)} %bitcast.5), calls=%async_computation.1 | async-start | bytes 32768 | tf_op jit(solution)/shard_map/all_to_all | solution.py:73
  1123.5 13.1 %all-to-all-start.2 = ((f32[32,1,8]{2,1,0:T(1,128)}), f32[32,1,8]{2,1,0:T(1,128)S(1)}, u32[]{:S(2)}, u32[]{:S(2)}) async-start(f32[32,1,8]{2,1,0:T(1,128)} %bitcast.6), calls=%async_computation.2 | async-start | bytes 32768 | tf_op jit(solution)/shard_map/all_to_all | solution.py:76
  1136.6 11.2 all-to-all-start
  1147.8 9.7 all-to-all-start.4
  1157.4 9.6 all-to-all-start.5
  1167.1 9.6 all-to-all-start.3
  1176.7 44.3 %all-to-all-start.6 = ((f32[32,1,160]{2,1,0:T(1,128)}), f32[32,1,160]{2,1,0:T(1,128)S(1)}, u32[]{:S(2)}, u32[]{:S(2)}) async-start(f32[32,1,160]{2,1,0:T(1,128)} %reshape.189), calls=%async_computation.6 | async-start | bytes 65536 | tf_op jit(solution)/shard_map/all_to_all | solution.py:82
  1221.0 12.2 all-to-all-start.7
Sparse Core Ops, SparseCore 0:
  10.8 63.1 all-gather.4
  76.9 59.0 all-gather.6
  187.7 251.5 all-reduce.2
where the time goes:
time: 1260 us; the launch traced here: 1250 us
  other arithmetic  627 us (50%)
  waiting for transfers between devices  406 us (32%)
  matrix products  105 us (8%)
  blocking collectives  40.4 us (3%)
  starting transfers between devices  29.9 us (2%)
  local copies, waits for them, and re-layouts  24.3 us (2%)
  between operations  14.5 us (1%)
    sort x4, other arithmetic, largest(): return lax.sort(values, dimension=values.ndim - 1)[..., -TOPK:]  604 us
    psum x1, waiting for transfers between devices, body(): lax.psum(jnp.dot(hidden_act, w_down, preferred_element_type=jnp.float32),...  251 us
    all_gather x2, waiting for transfers between devices, body(): lax.all_gather(own_rows, ('section', 'vocab'), axis=0, tiled=True)  123 us
    dot_general x2, matrix products, body(): logits = jnp.dot(scaled, head_weight, preferred_element_type=jnp.float32)  56.6 us
    psum x1, blocking collectives, body(): seq_logprob = lax.psum(jnp.stack(partials), ('section', 'vocab'))  40.4 us
    dot_general x2, matrix products, body(): jnp.dot(hidden_act, w_down, preferred_element_type=jnp.float32)  39 us
  transfers between devices with their start and end apart: 11, of which 9 were waited for; matrix products, arithmetic and copies ran while one was open for 53% of the time, Pallas kernels for 0%

commit v1 on v0

--- a/solution.py
+++ b/solution.py
@@ -52,9 +52,9 @@
         gate_proj = jnp.dot(normed, w_gate, preferred_element_type=jnp.float32)
         up_proj = jnp.dot(normed, w_up, preferred_element_type=jnp.float32)
         hidden_act = (jax.nn.silu(gate_proj) * up_proj).astype(jnp.bfloat16)
-        branch = lax.psum(
-            jnp.dot(hidden_act, w_down, preferred_element_type=jnp.float32), ("section", "vocab")
-        )
+        branch = jnp.dot(hidden_act, w_down, preferred_element_type=jnp.float32)
+        for k in ("vocab", "section"):
+            branch = jax.lax.psum(branch, k)
         residual = (gathered.astype(jnp.float32) + branch).astype(jnp.bfloat16)
         scaled = rms_norm(residual, gain_final)
         logits = jnp.dot(scaled, head_weight, preferred_element_type=jnp.float32)

time: 1260 us -> 1470 us (1.17)
  waiting for transfers between devices: 406 us -> 614 us
    psum x1 -> x2, waiting for transfers between devices: 251 us -> 459 us  [body(): branch = jax.lax.psum(branch, k)]
  transfers between devices with their start and end apart: 11 -> 12, of which waited for: 9 -> 10; matrix products, arithmetic and copies ran while one was open for 53% -> 24% of each run, Pallas kernels for 0% -> 0%
where the time goes in v1:
time: 1470 us; the launch traced here: 1460 us
  other arithmetic  627 us (43%)
  waiting for transfers between devices  614 us (42%)
  matrix products  105 us (7%)
  blocking collectives  40.4 us (3%)
  starting transfers between devices  31.2 us (2%)
  local copies, waits for them, and re-layouts  24.3 us (2%)
    sort x4, other arithmetic, largest(): return lax.sort(values, dimension=values.ndim - 1)[..., -TOPK:]  604 us
    psum x2, waiting for transfers between devices, body(): branch = jax.lax.psum(branch, k)  459 us
    all_gather x2, waiting for transfers between devices, body(): lax.all_gather(own_rows, ('section', 'vocab'), axis=0, tiled=True)  123 us
    dot_general x2, matrix products, body(): logits = jnp.dot(scaled, head_weight, preferred_element_type=jnp.float32)  56.4 us
    psum x1, blocking collectives, body(): seq_logprob = lax.psum(jnp.stack(partials), ('section', 'vocab'))  40.4 us
    dot_general x2, matrix products, body(): branch = jnp.dot(hidden_act, w_down, preferred_element_type=jnp.float32)  38.9 us
  transfers between devices with their start and end apart: 12, of which 10 were waited for; matrix products, arithmetic and copies ran while one was open for 24% of the time, Pallas kernels for 0%

profile of v1, /device:TPU:0, one launch (start us, length us, event | category | flops | bytes accessed | tf_op | source)
XLA Modules:
  0.0 1456.1 jit_solution(13081088662104461363)
XLA Ops:
  7.2 1.6 fusion.44
  8.9 0.7 all-gather.7.cloned.1.call-update
  9.7 64.3 %all-gather.5.cloned.1.call-done = bf16[1,256,7168]{2,1,0:T(8,128)(2,1)} async-done(((bf16[1,8,7168]{2,1,0:T(8,128)(2,1)}), bf16[1,256,7168]{2,1,0:T(8,128)(2,1)}) %all-gather.5.cloned.1.call-update) | async-done | bytes 3670032 | tf_op jit(solution)/shard_map/all_gather | solution.py:50
  74.0 2.8 fusion.6
  76.9 59.1 %all-gather.7.cloned.1.call-done = bf16[1,256,7168]{2,1,0:T(8,128)(2,1)} async-done(((bf16[1,8,7168]{2,1,0:T(8,128)(2,1)}), bf16[1,256,7168]{2,1,0:T(8,128)(2,1)}) %all-gather.7.cloned.1.call-update) | async-done | bytes 3670032 | tf_op jit(solution)/shard_map/all_gather | solution.py:50
  135.9 3.0 fusion.10
  139.0 7.0 fusion.28
  146.0 2.4 fusion.25
  148.5 19.6 %fusion.34 = f32[256,7168]{1,0:T(8,128)} fusion(bf16[576,7168]{1,0:T(8,128)(2,1)} %param.13, bf16[7168,576]{0,1:T(8,128)(2,1)} %param.12, bf16[1,256,7168]{2,1,0:T(8,128)(2,1)} %all-gather.5.cloned.1.call-done, f32[7168]{0:T(1024)S(1)} %copy-done.3, f32[256]{0:T(256)S(1)} %add_rsqrt_fusion.3, f32[256,576]{0,1:T(8,128)S(1)} %fusion.28), kind=kOutput, calls=%fused_computation.41 | convolution fusion | flops 4236083200 | bytes 28144640 | tf_op jit(solution)/shard_map/dot_general | solution.py:55
  168.0 19.4 %fusion.31 = f32[256,7168]{1,0:T(8,128)} fusion(bf16[576,7168]{1,0:T(8,128)(2,1)} %param.13, bf16[7168,576]{0,1:T(8,128)(2,1)} %param.12, bf16[1,256,7168]{2,1,0:T(8,128)(2,1)} %all-gather.7.cloned.1.call-done, f32[256]{0:T(256)S(1)} %add_rsqrt_fusion.1, f32[7168]{0:T(1024)S(1)} %copy-done.3, f32[256,576]{0,1:T(8,128)S(1)} %fusion.25), kind=kOutput, calls=%fused_computation.40 | convolution fusion | flops 4236083200 | bytes 28144640 | tf_op jit(solution)/shard_map/dot_general | solution.py:55
  187.9 404.8 %all-reduce.5.cloned.1.call-done = (f32[256,7168]{1,0:T(8,128)}, f32[256,7168]{1,0:T(8,128)}) async-done(((f32[256,7168]{1,0:T(8,128)}, f32[256,7168]{1,0:T(8,128)}), (f32[256,7168]{1,0:T(8,128)}, f32[256,7168]{1,0:T(8,128)})) %all-reduce.5.cloned.1.call-update) | async-done | bytes 14680080 | tf_op jit(solution)/shard_map/psum | solution.py:57
  593.5 54.3 %all-reduce.7.cloned.1.call-done = (f32[256,7168]{1,0:T(8,128)}, f32[256,7168]{1,0:T(8,128)}) async-done(((f32[256,7168]{1,0:T(8,128)}, f32[256,7168]{1,0:T(8,128)}), (f32[256,7168]{1,0:T(8,128)}, f32[256,7168]{1,0:T(8,128)})) %all-reduce.7.cloned.1.call-update) | async-done | bytes 14680080 | tf_op jit(solution)/shard_map/psum | solution.py:57
  647.8 8.4 fusion
  656.2 28.2 %fusion.46 = (f32[256]{0:T(256)S(1)}, f32[256,4040]{0,1:T(8,128)}) fusion(bf16[7168,4040]{0,1:T(8,128)(2,1)} %param.15, f32[7168]{0:T(1024)S(1)} %copy-done.4, f32[256]{0:T(256)S(1)} %add_rsqrt_fusion.2, f32[256,7168]{1,0:T(8,128)} %get-tuple-element.27, bf16[1,256,7168]{2,1,0:T(8,128)(2,1)} %all-gather.5.cloned.1.call-done), kind=kOutput, calls=%fused_computation.75 | convolution fusion | flops 14840743936 | bytes 73095168 | tf_op jit(solution)/shard_map/dot_general | solution.py:60
  684.3 2.3 iota.24.clone
  686.6 296.8 %sort.56 = (f32[256,4040]{0,1:T(8,128)}, s32[256,4040]{0,1:T(8,128)}) sort(f32[256,4040]{0,1:T(8,128)} %get-tuple-element.41, s32[256,4040]{0,1:T(8,128)} %iota.24.clone), dimensions={1}, to_apply=%region_20.21 | sort | flops 20684800 | bytes 16547840 | tf_op jit(solution)/shard_map/sort | solution.py:18
  983.5 5.6 copy.39
  989.0 0.7 all_to_all.52
  989.7 5.8 all-to-all-start.1
  995.5 28.2 %fusion.47 = (f32[256]{0:T(256)S(1)}, f32[256,4040]{0,1:T(8,128)}) fusion(bf16[7168,4040]{0,1:T(8,128)(2,1)} %param.15, f32[256]{0:T(256)S(1)} %add_rsqrt_fusion, f32[7168]{0:T(1024)S(1)} %copy-done.4, f32[256,7168]{1,0:T(8,128)} %get-tuple-element.26, bf16[1,256,7168]{2,1,0:T(8,128)(2,1)} %all-gather.7.cloned.1.call-done), kind=kOutput, calls=%fused_computation.76 | convolution fusion | flops 14840743936 | bytes 73095168 | tf_op jit(solution)/shard_map/dot_general | solution.py:60
  1023.7 5.1 exponential_reduce_fusion.1
  1028.8 1.0 slice_bitcast_fusion.1
  1029.8 296.8 %sort.58 = (f32[256,4040]{0,1:T(8,128)}, s32[256,4040]{0,1:T(8,128)}) sort(f32[256,4040]{0,1:T(8,128)} %get-tuple-element.43, s32[256,4040]{0,1:T(8,128)} %iota.24.clone), dimensions={1}, to_apply=%region_23.24 | sort | flops 20684800 | bytes 16547840 | tf_op jit(solution)/shard_map/sort | solution.py:18
  1326.6 0.7 all_to_all.54
  1327.3 5.5 copy.43
  1332.8 5.8 all-to-all-start.2
  1338.7 1.0 slice_bitcast_fusion
  1339.7 0.7 all_to_all.60
  1340.4 0.8 reshape.189
  1341.1 0.7 all_to_all.50
  1341.8 0.7 reshape.187
  1342.6 0.7 all_to_all.62
  1344.0 1.8 all-to-all-done.2
  1345.8 4.0 all-to-all-start
  1349.9 7.1 all-to-all-done
  1357.0 2.5 all-to-all-start.4
  1359.6 7.1 all-to-all-done.4
  1366.7 2.5 all-to-all-start.5
  1369.2 7.1 all-to-all-done.5
  1376.3 2.5 all-to-all-start.3
  1378.8 7.1 all-to-all-done.3
  1385.9 2.5 all-to-all-start.6
  1389.9 40.4 %psum.39 = f32[2,8]{1,0:T(2,128)} all-reduce(f32[2,8]{1,0:T(2,128)S(1)} %pad_maximum_fusion.3), channel_id=1, replica_groups=mesh['section'=2,'vocab'=16] {'section','vocab'}, use_global_device_ids=true, to_apply=%region_28.29 | all-reduce | flops 16 | bytes 128 | tf_op jit(solution)/shard_map/psum | solution.py:94
  1430.3 5.0 all-to-all-start.7
  1435.8 0.7 reduce.5
  1436.8 4.9 sort.57
  1442.5 0.7 reduce.4
  1443.5 4.9 sort.59
  (60 shorter events, 6.2 us)
Async XLA Ops:
  7.2 131.8 %copy-start.3 = (f32[7168]{0:T(1024)S(1)}, f32[7168]{0:T(1024)}, u32[]{:S(2)}) copy-start(f32[7168]{0:T(1024)} %param.10) | copy-start | bytes 86020
  7.2 66.8 %all-gather.5.cloned.1.call-start = ((), (), s32[]{:S(2)}) async-start(), calls=%async_computation.8 | async-start | bytes 3784704 | tf_op jit(solution)/shard_map/all_gather | solution.py:50
  8.9 127.0 %all-gather.7.cloned.1.call-start = ((), (), s32[]{:S(2)}) async-start(), calls=%async_computation.9 | async-start | bytes 3784704 | tf_op jit(solution)/shard_map/all_gather | solution.py:50
  9.6 583.1 %all-reduce.5.cloned.1.call-start = ((), (), s32[]{:S(2)}) async-start(), calls=%async_computation.10 | async-start | bytes 29360128 | tf_op jit(solution)/shard_map/psum | solution.py:57
  135.9 10.1 slice-start
  138.9 7.1 copy-start
  139.0 7.1 slice-start.1
  187.4 460.3 %all-reduce.7.cloned.1.call-start = ((), (), s32[]{:S(2)}) async-start(), calls=%async_computation.11 | async-start | bytes 29360128 | tf_op jit(solution)/shard_map/psum | solution.py:57
  592.8 0.7 copy-start.2
  592.8 0.7 copy-start.1
  647.8 8.4 copy-start.4
  989.7 343.1 %all-to-all-start.1 = ((f32[32,1,8]{2,1,0:T(1,128)}), f32[32,1,8]{2,1,0:T(1,128)S(1)}, u32[]{:S(2)}, u32[]{:S(2)}) async-start(f32[32,1,8]{2,1,0:T(1,128)} %bitcast.5), calls=%async_computation.1 | async-start | bytes 32768 | tf_op jit(solution)/shard_map/all_to_all | solution.py:73
  1332.8 13.0 all-to-all-start.2
  1345.8 11.2 all-to-all-start
  1357.0 9.7 all-to-all-start.4
  1366.7 9.6 all-to-all-start.5
  1376.3 9.6 all-to-all-start.3
  1385.9 44.3 %all-to-all-start.6 = ((f32[32,1,160]{2,1,0:T(1,128)}), f32[32,1,160]{2,1,0:T(1,128)S(1)}, u32[]{:S(2)}, u32[]{:S(2)}) async-start(f32[32,1,160]{2,1,0:T(1,128)} %reshape.189), calls=%async_computation.6 | async-start | bytes 65536 | tf_op jit(solution)/shard_map/all_to_all | solution.py:82
  1430.3 12.2 all-to-all-start.7
Sparse Core Ops, SparseCore 0:
  10.8 63.1 all-gather.4
  76.9 59.0 all-gather.6
  187.5 405.1 all-reduce.4
  595.2 52.5 all-reduce.6
